TPU v7x, 256 devices: a whole 4x4x8 slice. The times are simulated.
256 devices in a mesh: grid: 32 (over y, x, core), rows: 8 (over z).
Axes of the slice: x: 4, y: 4, z: 8, core: 2. Of those that a mesh axis runs over, the one named last changes fastest.
Arguments:
- density: bfloat16 [32, 128, 4096], P(None, 'rows', 'grid'), as said below
- basis_values: bfloat16 [64, 16, 128, 512], P('grid', None, 'rows'), may hold values from -0.59765625 to 0.59765625
- grid_points: float32 [64, 3, 512], P('grid'), may hold values from -4 to 4
- grid_weights: float32 [64, 512], P('grid'), may hold values from 0.05 to 1
- screened_blocks: int32 [64, 16], P('grid'), may hold values from 0 to 31, as said below
Outputs:
- exchange: float32 [32, 128, 4096], P(None, 'rows', 'grid')
Inputs may be any that keep to these rules, and one draw needn't show every extreme that they name: density is symmetric: density[a, i, b * 128 + j] equals density[b, j, a * 128 + i]. `screened_blocks`: each row holds 16 distinct block numbers.
All inputs are finite; a program needn't handle non-finite values.
Results may differ from a plain program's by a relative error of at most 0.00055.
The roundings to bfloat16 on the way count: a program that leaves them out, or rounds other values in their place, can miss the bound.
Values may be sent and summed in bfloat16 or wider, within the bound.
A program may use at most 64 MiB of HBM per device.

v0:
```python
import jax
import jax.numpy as jnp
from jax import lax
from jax.sharding import PartitionSpec as P


def copy_for_each(shard, axis):
    copies = jnp.broadcast_to(shard, (lax.axis_size(axis), *shard.shape))
    return lax.all_to_all(copies, axis, split_axis=0, concat_axis=0, tiled=True)


def joined_along(blocks, dim):
    shape = list(blocks.shape[1:])
    shape[dim] *= blocks.shape[0]
    return jnp.moveaxis(blocks, 0, dim).reshape(shape)


def gather_directly(shard, axis, dim):
    blocks = copy_for_each(shard, axis)
    return joined_along(blocks, dim)


def body(density, basis_values, grid_points, grid_weights, screened_blocks):
    nblocks = density.shape[0]
    rows_mine = density.shape[1]
    block_size = rows_mine * lax.axis_size("rows")
    nbasis = nblocks * block_size
    nsig = basis_values.shape[1]
    npoints = basis_values.shape[3]
    stripe = lax.all_gather(density, "grid", axis=2, tiled=True)
    totals = jnp.zeros((nblocks, rows_mine, nblocks, block_size), jnp.float32)
    for batch_index in range(basis_values.shape[0]):
        blocks = screened_blocks[batch_index]
        row_pick = jnp.take(stripe, blocks, axis=0).reshape(nsig * rows_mine, nblocks, block_size)
        chosen = jnp.take(row_pick, blocks, axis=1)
        local_values = basis_values[batch_index]
        x_mine = local_values.reshape(nsig * rows_mine, npoints)
        fsum = jnp.einsum(
            "mtk,tkp->mp",
            chosen,
            gather_directly(local_values, "rows", 1),
            preferred_element_type=jnp.float32,
        )
        fmat = fsum.astype(jnp.bfloat16)
        intersection_part = lax.dot_general(
            x_mine, fmat, (((0,), (0,)), ((), ())), preferred_element_type=jnp.float32
        )
        intersection = lax.psum(intersection_part, "rows")
        places = grid_points[batch_index]
        weights = grid_weights[batch_index]
        diffs = places[:, :, None] - places[:, None, :]
        kern = 1.0 / jnp.sqrt(jnp.sum(diffs * diffs, axis=0) + 0.5)
        mixed = (weights[:, None] * kern * intersection).astype(jnp.bfloat16)
        potential = (
            jnp.dot(x_mine, mixed, preferred_element_type=jnp.float32) * weights[None, :]
        ).astype(jnp.bfloat16)
        potential = potential.reshape(nsig, rows_mine, npoints)
        block_k = jnp.einsum(
            "mp,tkp->mtk",
            x_mine,
            lax.all_gather(potential, "rows", axis=1, tiled=True),
            preferred_element_type=jnp.float32,
        )
        block_k = block_k.reshape(nsig, rows_mine, nsig, block_size)
        totals = totals.at[blocks[:, None], :, blocks[None, :], :].add(
            block_k.transpose(0, 2, 1, 3)
        )
    return lax.psum_scatter(
        totals.reshape(nblocks, rows_mine, nbasis), "grid", scatter_dimension=2, tiled=True
    )


def solution(mesh):
    placed = (
        P(None, "rows", "grid"),
        P("grid", None, "rows", None),
        P("grid", None, None),
        P("grid", None),
        P("grid", None),
    )
    return jax.shard_map(
        body, mesh=mesh, in_specs=placed, out_specs=P(None, "rows", "grid"), check_vma=False
    )
```

profile of v0, /device:TPU:2, one launch (start us, length us, event | category | flops | bytes accessed | tf_op | source)
XLA Modules:
  0.0 494.6 jit_solution(1196830963108560420)
XLA Ops:
  6.5 0.0 all-gather.4.cloned.1.call-start
  6.5 0.7 all-gather.4.cloned.1.call-update
  7.3 1.1 slice_bitcast_fusion
  8.4 0.3 broadcast_in_dim.59
  8.6 59.6 %all_to_all.10 = bf16[8,16,16,512]{3,2,1,0:T(8,128)(2,1)} all-to-all(bf16[8,16,16,512]{3,2,1,0:T(8,128)(2,1)S(1)} %broadcast_in_dim.59), channel_id=1, replica_groups=mesh['grid'=32,'rows'=8] {'rows'}, dimensions={0} | all-to-all | bytes 4194304 | tf_op jit(solution)/shard_map/all_to_all | solution.py:9
  68.2 1.6 broadcast_in_dim.55
  69.8 0.0 copy-start.3
  69.8 3.7 all-to-all-start
  73.5 0.0 all-reduce.3.cloned.1.call-start
  73.6 0.0 copy-done.3
  73.7 3.2 copy.34
  76.8 46.5 %all-to-all-done = bf16[8,16,16,512]{3,2,1,0:T(8,128)(2,1)S(1)} async-done(((bf16[8,16,16,512]{3,2,1,0:T(8,128)(2,1)}), bf16[8,16,16,512]{3,2,1,0:T(8,128)(2,1)S(1)}, u32[]{:S(2)}, u32[]{:S(2)}) %all-to-all-start) | async-done | bytes 2097184 | tf_op jit(solution)/shard_map/all_to_all | solution.py:9
  123.3 1.6 copy.29
  124.9 0.0 all-gather.4.cloned.1.call-done
  124.9 2.9 gather_fusion.2
  127.8 0.3 broadcast_select_fusion
  128.0 0.5 copy.42
  128.5 0.8 copy.33
  129.3 1.7 gather_fusion.3
  131.1 2.9 gather_fusion
  134.0 0.3 broadcast_select_fusion.1
  134.2 0.5 copy.41
  134.7 0.8 copy.28
  135.5 1.7 gather_fusion.1
  137.2 0.0 copy-start
  137.2 4.1 convolution_bitcast_fusion.2
  141.3 0.0 copy-done
  141.3 3.3 convolution_bitcast_fusion.3
  144.6 0.0 copy-start.1
  144.6 0.0 all-reduce.3.cloned.1.call-update
  144.6 0.0 copy-start.2
  144.6 0.0 all-gather.6.cloned.1.call-start
  144.6 0.6 copy-done.1
  145.3 0.4 multiply_reduce_fusion.1
  145.7 0.3 copy.27
  146.0 0.0 copy-done.2
  146.0 77.3 %all-reduce.3.cloned.1.call-done = (f32[512,512]{0,1:T(8,128)}, f32[512,512]{0,1:T(8,128)}) async-done(((f32[512,512]{0,1:T(8,128)}, f32[512,512]{0,1:T(8,128)}), (f32[512,512]{0,1:T(8,128)}, f32[512,512]{0,1:T(8,128)})) %all-reduce.3.cloned.1.call-update) | async-done | bytes 2097168 | tf_op jit(solution)/shard_map/psum | solution.py:48
  223.3 2.3 fusion
  225.6 0.0 all-gather.6.cloned.1.call-update
  225.7 0.0 all-gather.8.cloned.1.call-start
  225.7 0.4 multiply_reduce_fusion
  226.1 0.3 copy.32
  226.4 2.3 fusion.1
  228.7 0.0 all-gather.8.cloned.1.call-update
  228.7 0.2 reduce-scatter.2.cloned.1.call-start
  229.0 0.1 or_select_fusion
  229.1 0.1 reshape.140
  229.2 0.1 reshape.146
  229.3 36.4 %all-gather.6.cloned.1.call-done = bf16[16,128,512]{2,1,0:T(8,128)(2,1)} async-done(((bf16[16,16,512]{2,1,0:T(8,128)(2,1)}), bf16[16,128,512]{2,1,0:T(8,128)(2,1)}) %all-gather.6.cloned.1.call-update) | async-done | bytes 2097168 | tf_op jit(solution)/shard_map/all_gather | solution.py:61
  265.7 2.3 convolution_bitcast_fusion.1
  268.0 2.0 copy.30
  270.0 2.3 copy.31
  272.2 34.5 %all-gather.8.cloned.1.call-done = bf16[16,128,512]{2,1,0:T(8,128)(2,1)} async-done(((bf16[16,16,512]{2,1,0:T(8,128)(2,1)}), bf16[16,128,512]{2,1,0:T(8,128)(2,1)}) %all-gather.8.cloned.1.call-update) | async-done | bytes 2097168 | tf_op jit(solution)/shard_map/all_gather | solution.py:61
  306.8 3.6 convolution_bitcast_fusion
  310.4 3.1 copy.35
  313.5 3.6 copy.36
  317.1 4.2 broadcast_in_dim.51
  321.3 28.4 %scatter_fusion = f32[32,16,32,128]{3,1,2,0:T(8,128)} fusion(f32[32,16,32,128]{3,1,2,0:T(8,128)} %broadcast_in_dim.51, s32[256]{0:T(256)S(1)} %reshape.140, f32[256,16,128]{2,1,0:T(8,128)S(1)} %bitcast.107), kind=kCustom, calls=%fused_computation.4 | custom fusion | flops 524288 | bytes 6293504 | tf_op jit(solution)/shard_map/scatter-add | solution.py:65
  349.7 31.8 %scatter_fusion.1 = f32[32,16,32,128]{3,1,2,0:T(8,128)} fusion(f32[32,16,32,128]{3,1,2,0:T(8,128)} %scatter_fusion, s32[256]{0:T(256)S(1)} %reshape.146, f32[256,16,128]{2,1,0:T(8,128)} %bitcast.108), kind=kCustom, calls=%fused_computation.5 | custom fusion | flops 524288 | bytes 6293504 | tf_op jit(solution)/shard_map/scatter-add | solution.py:65
  381.5 7.8 %copy_bitcast_fusion = f32[32,16,4096]{2,1,0:T(8,128)} fusion(f32[32,16,32,128]{3,1,2,0:T(8,128)} %scatter_fusion.1), kind=kLoop, calls=%fused_computation.6 | loop fusion | bytes 16777216 | tf_op jit(solution)/shard_map/reshape | solution.py:69
  389.2 0.0 reduce-scatter.2.cloned.1.call-update
  389.3 98.8 %reduce-scatter.2.cloned.1.call-done = f32[32,16,128]{2,1,0:T(8,128)} async-done(((f32[32,16,4096]{2,1,0:T(8,128)}), f32[32,16,128]{2,1,0:T(8,128)}) %reduce-scatter.2.cloned.1.call-update) | async-done | bytes 262160 | tf_op jit(solution)/shard_map/reduce_scatter | solution.py:68
  (11 shorter events, 0.1 us)
Async XLA Ops:
  6.5 118.4 %all-gather.4.cloned.1.call-start = ((), (), s32[]{:S(2)}) async-start(), calls=%async_computation.3 | async-start | bytes 4325376 | tf_op jit(solution)/shard_map/all_gather | solution.py:30
  69.8 3.8 copy-start.3
  69.8 53.5 %all-to-all-start = ((bf16[8,16,16,512]{3,2,1,0:T(8,128)(2,1)}), bf16[8,16,16,512]{3,2,1,0:T(8,128)(2,1)S(1)}, u32[]{:S(2)}, u32[]{:S(2)}) async-start(bf16[8,16,16,512]{3,2,1,0:T(8,128)(2,1)} %broadcast_in_dim.55), calls=%async_computation | async-start | bytes 4194304 | tf_op jit(solution)/shard_map/all_to_all | solution.py:9
  73.5 149.8 %all-reduce.3.cloned.1.call-start = ((), (), s32[]{:S(2)}) async-start(), calls=%async_computation.7 | async-start | bytes 4194304 | tf_op jit(solution)/shard_map/psum | solution.py:48
  137.2 4.1 copy-start
  144.6 0.7 copy-start.1
  144.6 1.4 copy-start.2
  144.6 121.1 %all-gather.6.cloned.1.call-start = ((), (), s32[]{:S(2)}) async-start(), calls=%async_computation.4 | async-start | bytes 2359296 | tf_op jit(solution)/shard_map/all_gather | solution.py:61
  225.7 81.1 %all-gather.8.cloned.1.call-start = ((), (), s32[]{:S(2)}) async-start(), calls=%async_computation.5 | async-start | bytes 2359296 | tf_op jit(solution)/shard_map/all_gather | solution.py:61
  228.7 259.3 %reduce-scatter.2.cloned.1.call-start = ((), (), s32[]{:S(2)}) async-start(), calls=%async_computation.6 | async-start | bytes 8650752 | tf_op jit(solution)/shard_map/reduce_scatter | solution.py:68
Sparse Core Ops, SparseCore 0:
  9.8 56.2 all-gather.3
  144.7 78.5 all-reduce.2
  225.8 39.8 all-gather.5
  267.3 39.4 all-gather.7
  389.4 98.5 reduce-scatter.1
where the time goes:
time: 496 us; the launch traced here: 495 us
  waiting for transfers between devices  294 us (59%)
  other arithmetic  61.6 us (12%)
  blocking collectives  59.6 us (12%)
  local copies, waits for them, and re-layouts  43.8 us (9%)
  matrix products  17.9 us (4%)
  between operations  13.4 us (3%)
    reduce_scatter x1, waiting for transfers between devices, body(): lax.psum_scatter(totals.reshape(nblocks, rows_mine, nbasis), 'grid', scat...  98.8 us
    psum x1, waiting for transfers between devices, body(): intersection = lax.psum(intersection_part, 'rows')  77.3 us
    all_gather x2, waiting for transfers between devices, body(): lax.all_gather(potential, 'rows', axis=1, tiled=True)  70.9 us
    scatter-add x2, other arithmetic, body(): totals.at[blocks[:, None], :, blocks[None, :], :]  60.2 us
    all_to_all x1, blocking collectives, copy_for_each(): return lax.all_to_all(copies, axis, split_axis=0, concat_axis=0, tiled=True)  59.6 us
    all_to_all x1, waiting for transfers between devices, copy_for_each(): return lax.all_to_all(copies, axis, split_axis=0, concat_axis=0, tiled=True)  46.5 us
  transfers between devices with their start and end apart: 6, of which 5 were waited for; matrix products, arithmetic and copies ran while one was open for 4% of the time, Pallas kernels for 0%

commit v1 on v0

--- a/solution.py
+++ b/solution.py
@@ -2,6 +2,19 @@
 import jax.numpy as jnp
 from jax import lax
 from jax.sharding import PartitionSpec as P
+
+
+def collect(x, axis, dim):
+    ways = lax.axis_size(axis)
+    up = [(d, (d + 1) % ways) for d in range(ways)]
+    down = [(d, (d - 1) % ways) for d in range(ways)]
+    earlier, later = ([x], [x])
+    for _ in range(ways // 2):
+        earlier.append(lax.ppermute(earlier[-1], axis, up))
+    for _ in range((ways - 1) // 2):
+        later.append(lax.ppermute(later[-1], axis, down))
+    line = jnp.concatenate([*earlier[::-1], *later[1:]], axis=dim)
+    return jnp.roll(line, (lax.axis_index(axis) - ways // 2) * x.shape[dim], axis=dim)
 
 
 def copy_for_each(shard, axis):
@@ -56,10 +69,7 @@
         ).astype(jnp.bfloat16)
         potential = potential.reshape(nsig, rows_mine, npoints)
         block_k = jnp.einsum(
-            "mp,tkp->mtk",
-            x_mine,
-            lax.all_gather(potential, "rows", axis=1, tiled=True),
-            preferred_element_type=jnp.float32,
+            "mp,tkp->mtk", x_mine, collect(potential, "rows", 1), preferred_element_type=jnp.float32
         )
         block_k = block_k.reshape(nsig, rows_mine, nsig, block_size)
         totals = totals.at[blocks[:, None], :, blocks[None, :], :].add(

time: 496 us -> 475 us (0.958)
  waiting for transfers between devices: 294 us -> 247 us
  starting transfers between devices: 4.08 us -> 23.7 us
  local copies, waits for them, and re-layouts: 43.8 us -> 53.5 us
    all_gather x2 -> x0, waiting for transfers between devices: 70.9 us -> none  [body(): lax.all_gather(potential, 'rows', axis=1, tiled=True)]
    ppermute x0 -> x14, waiting for transfers between devices: none -> 24.9 us  [the longest x8 24.5 us: collect(): earlier.append(lax.ppermute(earlier[-1], axis, up))]
    ppermute x0 -> x14, starting transfers between devices: none -> 19.9 us  [the longest x6 17.2 us: collect(): later.append(lax.ppermute(later[-1], axis, down))]
    unnamed x11 -> x41, local copies, waits for them, and re-layouts: 1.59 us -> 9.81 us
  transfers between devices with their start and end apart: 6 -> 18, of which waited for: 5 -> 10; matrix products, arithmetic and copies ran while one was open for 4% -> 5% of each run, Pallas kernels for 0% -> 0%
where the time goes in v1:
time: 475 us; the launch traced here: 474 us
  waiting for transfers between devices  247 us (52%)
  other arithmetic  61.6 us (13%)
  blocking collectives  59.6 us (13%)
  local copies, waits for them, and re-layouts  53.5 us (11%)
  starting transfers between devices  23.7 us (5%)
  matrix products  14.2 us (3%)
  between operations  13.5 us (3%)
    reduce_scatter x1, waiting for transfers between devices, body(): lax.psum_scatter(totals.reshape(nblocks, rows_mine, nbasis), 'grid', scat...  98.8 us
    psum x1, waiting for transfers between devices, body(): intersection = lax.psum(intersection_part, 'rows')  76.6 us
    scatter-add x2, other arithmetic, body(): totals.at[blocks[:, None], :, blocks[None, :], :]  60.2 us
    all_to_all x1, blocking collectives, copy_for_each(): return lax.all_to_all(copies, axis, split_axis=0, concat_axis=0, tiled=True)  59.6 us
    all_to_all x1, waiting for transfers between devices, copy_for_each(): return lax.all_to_all(copies, axis, split_axis=0, concat_axis=0, tiled=True)  46.5 us
    ppermute x8, waiting for transfers between devices, collect(): earlier.append(lax.ppermute(earlier[-1], axis, up))  24.5 us
    ppermute x6, starting transfers between devices, collect(): later.append(lax.ppermute(later[-1], axis, down))  17.2 us
    unnamed x41, local copies, waits for them, and re-layouts  9.81 us
  transfers between devices with their start and end apart: 18, of which 10 were waited for; matrix products, arithmetic and copies ran while one was open for 5% of the time, Pallas kernels for 0%

profile of v1, /device:TPU:2, one launch (start us, length us, event | category | flops | bytes accessed | tf_op | source)
XLA Modules:
  0.0 473.5 jit_solution(90318318561913558)
XLA Ops:
  6.5 0.7 all-gather.2.cloned.1.call-update
  7.3 1.8 slice_bitcast_fusion
  9.1 0.3 broadcast_in_dim.55
  9.3 59.6 %all_to_all.10 = bf16[8,16,16,512]{3,2,1,0:T(8,128)(2,1)} all-to-all(bf16[8,16,16,512]{3,2,1,0:T(8,128)(2,1)S(1)} %broadcast_in_dim.55), channel_id=1, replica_groups=mesh['grid'=32,'rows'=8] {'rows'}, dimensions={0} | all-to-all | bytes 4194304 | tf_op jit(solution)/shard_map/all_to_all | solution.py:22
  68.9 1.7 broadcast_in_dim.59
  70.5 3.7 all-to-all-start.1
  74.4 3.2 copy.29
  77.6 46.5 %all-to-all-done.1 = bf16[8,16,16,512]{3,2,1,0:T(8,128)(2,1)S(1)} async-done(((bf16[8,16,16,512]{3,2,1,0:T(8,128)(2,1)}), bf16[8,16,16,512]{3,2,1,0:T(8,128)(2,1)S(1)}, u32[]{:S(2)}, u32[]{:S(2)}) %all-to-all-start.1) | async-done | bytes 2097184 | tf_op jit(solution)/shard_map/all_to_all | solution.py:22
  124.1 1.6 copy.34
  125.7 2.9 gather_fusion
  128.6 0.3 broadcast_select_fusion.1
  128.8 0.5 copy.41
  129.3 0.8 copy.28
  130.1 0.7 gather_fusion.1
  130.9 2.9 gather_fusion.2
  133.8 0.3 broadcast_select_fusion
  134.1 0.5 copy.42
  134.5 0.8 copy.33
  135.4 1.6 gather_fusion.3
  137.0 3.8 convolution_bitcast_fusion.1
  140.8 3.3 convolution_bitcast_fusion
  144.2 0.6 copy-done.9
  144.8 0.4 multiply_reduce_fusion.1
  145.2 0.3 copy.27
  145.5 0.4 multiply_reduce_fusion
  145.9 0.3 copy.32
  146.3 76.6 %all-reduce.3.cloned.1.call-done = (f32[512,512]{0,1:T(8,128)}, f32[512,512]{0,1:T(8,128)}) async-done(((f32[512,512]{0,1:T(8,128)}, f32[512,512]{0,1:T(8,128)}), (f32[512,512]{0,1:T(8,128)}, f32[512,512]{0,1:T(8,128)})) %all-reduce.3.cloned.1.call-update) | async-done | bytes 2097168 | tf_op jit(solution)/shard_map/psum | solution.py:61
  222.8 1.7 fusion.12
  224.6 1.1 collective-permute-start
  225.7 0.4 fusion.13
  226.0 1.4 collective-permute-start.7
  227.4 7.3 %collective-permute-done = bf16[16,16,512]{2,1,0:T(8,128)(2,1)S(1)} collective-permute-done((bf16[16,16,512]{2,1,0:T(8,128)(2,1)S(1)}, bf16[16,16,512]{2,1,0:T(8,128)(2,1)S(1)}, u32[]{:S(2)}, u32[]{:S(2)}) %collective-permute-start) | collective-permute-done | bytes 262176 | tf_op jit(solution)/shard_map/ppermute | solution.py:13
  234.8 3.2 collective-permute-start.4
  238.0 2.4 collective-permute-done.7
  240.5 5.6 %collective-permute-done.1 = bf16[16,16,512]{2,1,0:T(8,128)(2,1)S(1)} collective-permute-done((bf16[16,16,512]{2,1,0:T(8,128)(2,1)S(1)}, bf16[16,16,512]{2,1,0:T(8,128)(2,1)S(1)}, u32[]{:S(2)}, u32[]{:S(2)}) %collective-permute-start.1) | collective-permute-done | bytes 262176 | tf_op jit(solution)/shard_map/ppermute | solution.py:13
  246.1 3.3 collective-permute-start.5
  249.3 0.4 collective-permute-done.11
  249.7 3.7 collective-permute-start.12
  253.4 3.8 collective-permute-done.2
  257.5 0.1 reshape.146
  257.6 3.3 collective-permute-start.6
  260.9 3.8 collective-permute-start.13
  264.7 1.9 collective-permute-done.3
  266.6 1.0 constant_dynamic-update-slice_fusion.7
  267.8 1.1 fusion.6
  268.9 3.5 collective-permute-done.10
  272.5 0.7 constant_dynamic-update-slice_fusion.15
  273.2 1.7 constant_dynamic-update-slice_fusion.14
  274.9 0.7 constant_dynamic-update-slice_fusion.13
  275.6 0.7 constant_dynamic-update-slice_fusion.12
  276.4 0.8 constant_dynamic-update-slice_fusion.11
  277.1 1.9 copy.30
  279.1 2.3 copy.31
  281.4 0.7 constant_dynamic-update-slice_fusion.10
  282.1 1.7 constant_dynamic-update-slice_fusion.9
  283.8 1.7 constant_dynamic-update-slice_fusion.8
  285.5 3.9 fusion.9
  289.4 3.0 copy.35
  292.4 3.6 copy.36
  296.0 4.2 broadcast_in_dim.51
  300.3 28.4 %scatter_fusion = f32[32,16,32,128]{3,1,2,0:T(8,128)} fusion(f32[32,16,32,128]{3,1,2,0:T(8,128)} %broadcast_in_dim.51, s32[256]{0:T(256)S(1)} %reshape.140, f32[256,16,128]{2,1,0:T(8,128)S(1)} %bitcast.105), kind=kCustom, calls=%fused_computation.4 | custom fusion | flops 524288 | bytes 6293504 | tf_op jit(solution)/shard_map/scatter-add | solution.py:75
  328.7 31.8 %scatter_fusion.1 = f32[32,16,32,128]{3,1,2,0:T(8,128)} fusion(f32[32,16,32,128]{3,1,2,0:T(8,128)} %scatter_fusion, s32[256]{0:T(256)S(1)} %reshape.146, f32[256,16,128]{2,1,0:T(8,128)} %bitcast.106), kind=kCustom, calls=%fused_computation.5 | custom fusion | flops 524288 | bytes 6293504 | tf_op jit(solution)/shard_map/scatter-add | solution.py:75
  360.5 7.7 %copy_bitcast_fusion = f32[32,16,4096]{2,1,0:T(8,128)} fusion(f32[32,16,32,128]{3,1,2,0:T(8,128)} %scatter_fusion.1), kind=kLoop, calls=%fused_computation.6 | loop fusion | bytes 16777216 | tf_op jit(solution)/shard_map/reshape | solution.py:79
  368.3 98.8 %reduce-scatter.2.cloned.1.call-done = f32[32,16,128]{2,1,0:T(8,128)} async-done(((f32[32,16,4096]{2,1,0:T(8,128)}), f32[32,16,128]{2,1,0:T(8,128)}) %reduce-scatter.2.cloned.1.call-update) | async-done | bytes 262160 | tf_op jit(solution)/shard_map/reduce_scatter | solution.py:78
  (63 shorter events, 0.9 us)
Async XLA Ops:
  6.5 119.2 %all-gather.2.cloned.1.call-start = ((), (), s32[]{:S(2)}) async-start(), calls=%async_computation.3 | async-start | bytes 4325376 | tf_op jit(solution)/shard_map/all_gather | solution.py:43
  70.5 3.8 copy-start.11
  70.5 53.5 %all-to-all-start.1 = ((bf16[8,16,16,512]{3,2,1,0:T(8,128)(2,1)}), bf16[8,16,16,512]{3,2,1,0:T(8,128)(2,1)S(1)}, u32[]{:S(2)}, u32[]{:S(2)}) async-start(bf16[8,16,16,512]{3,2,1,0:T(8,128)(2,1)} %broadcast_in_dim.59), calls=%async_computation.1 | async-start | bytes 4194304 | tf_op jit(solution)/shard_map/all_to_all | solution.py:22
  74.3 148.5 %all-reduce.3.cloned.1.call-start = ((), (), s32[]{:S(2)}) async-start(), calls=%async_computation.5 | async-start | bytes 4194304 | tf_op jit(solution)/shard_map/psum | solution.py:61
  137.0 3.8 copy-start
  144.1 0.7 copy-start.9
  144.1 322.9 %reduce-scatter.2.cloned.1.call-start = ((), (), s32[]{:S(2)}) async-start(), calls=%async_computation.4 | async-start | bytes 8650752 | tf_op jit(solution)/shard_map/reduce_scatter | solution.py:78
  145.5 0.7 copy-start.10
  222.8 2.8 copy-start.1
  224.6 10.2 %collective-permute-start = (bf16[16,16,512]{2,1,0:T(8,128)(2,1)S(1)}, bf16[16,16,512]{2,1,0:T(8,128)(2,1)S(1)}, u32[]{:S(2)}, u32[]{:S(2)}) collective-permute-start(bf16[16,16,512]{2,1,0:T(8,128)(2,1)S(1)} %bitcast.118), channel_id=1, source_target_pairs={{0,1},{1,2},{2,3},{3,4},{4,5},{5,6},{6,7},{7,0},{8,9},{9,10},{10,1... | collective-permute-start | bytes 786440 | tf_op jit(solution)/shard_map/ppermute | solution.py:13
  226.0 14.4 %collective-permute-start.7 = (bf16[16,16,512]{2,1,0:T(8,128)(2,1)S(1)}, bf16[16,16,512]{2,1,0:T(8,128)(2,1)S(1)}, u32[]{:S(2)}, u32[]{:S(2)}) collective-permute-start(bf16[16,16,512]{2,1,0:T(8,128)(2,1)S(1)} %bitcast.115), channel_id=1, source_target_pairs={{0,1},{1,2},{2,3},{3,4},{4,5},{5,6},{6,7},{7,0},{8,9},{9,10},{10,1... | collective-permute-start | bytes 786440 | tf_op jit(solution)/shard_map/ppermute | solution.py:13
  234.8 11.2 %collective-permute-start.1 = (bf16[16,16,512]{2,1,0:T(8,128)(2,1)S(1)}, bf16[16,16,512]{2,1,0:T(8,128)(2,1)S(1)}, u32[]{:S(2)}, u32[]{:S(2)}) collective-permute-start(bf16[16,16,512]{2,1,0:T(8,128)(2,1)S(1)} %collective-permute-done), channel_id=1, source_target_pairs={{0,1},{1,2},{2,3},{3,4},{4,5},{5,6},{6,7},{7,0},{8,9},{9,10},{10,1... | collective-permute-start | bytes 786440 | tf_op jit(solution)/shard_map/ppermute | solution.py:13
  234.8 11.3 %collective-permute-start.4 = (bf16[16,16,512]{2,1,0:T(8,128)(2,1)S(1)}, bf16[16,16,512]{2,1,0:T(8,128)(2,1)S(1)}, u32[]{:S(2)}, u32[]{:S(2)}) collective-permute-start(bf16[16,16,512]{2,1,0:T(8,128)(2,1)S(1)} %bitcast.119), channel_id=1, source_target_pairs={{0,7},{1,0},{2,1},{3,2},{4,3},{5,4},{6,5},{7,6},{8,15},{9,8},{10,9... | collective-permute-start | bytes 786440 | tf_op jit(solution)/shard_map/ppermute | solution.py:15
  238.0 11.7 %collective-permute-start.11 = (bf16[16,16,512]{2,1,0:T(8,128)(2,1)S(1)}, bf16[16,16,512]{2,1,0:T(8,128)(2,1)S(1)}, u32[]{:S(2)}, u32[]{:S(2)}) collective-permute-start(bf16[16,16,512]{2,1,0:T(8,128)(2,1)S(1)} %bitcast.116), channel_id=1, source_target_pairs={{0,7},{1,0},{2,1},{3,2},{4,3},{5,4},{6,5},{7,6},{8,15},{9,8},{10,9... | collective-permute-start | bytes 786440 | tf_op jit(solution)/shard_map/ppermute | solution.py:15
  240.4 17.2 %copy-start.3 = (bf16[16,16,512]{2,1,0:T(8,128)(2,1)}, bf16[16,16,512]{2,1,0:T(8,128)(2,1)S(1)}, u32[]{:S(2)}) copy-start(bf16[16,16,512]{2,1,0:T(8,128)(2,1)S(1)} %collective-permute-done.7) | copy-start | bytes 786436
  240.4 13.0 %collective-permute-start.8 = (bf16[16,16,512]{2,1,0:T(8,128)(2,1)S(1)}, bf16[16,16,512]{2,1,0:T(8,128)(2,1)S(1)}, u32[]{:S(2)}, u32[]{:S(2)}) collective-permute-start(bf16[16,16,512]{2,1,0:T(8,128)(2,1)S(1)} %collective-permute-done.7), channel_id=1, source_target_pairs={{0,1},{1,2},{2,3},{3,4},{4,5},{5,6},{6,7},{7,0},{8,9},{9,10},{10,1... | collective-permute-start | bytes 786440 | tf_op jit(solution)/shard_map/ppermute | solution.py:13
  246.0 11.2 %collective-permute-start.2 = (bf16[16,16,512]{2,1,0:T(8,128)(2,1)S(1)}, bf16[16,16,512]{2,1,0:T(8,128)(2,1)S(1)}, u32[]{:S(2)}, u32[]{:S(2)}) collective-permute-start(bf16[16,16,512]{2,1,0:T(8,128)(2,1)S(1)} %collective-permute-done.1), channel_id=1, source_target_pairs={{0,1},{1,2},{2,3},{3,4},{4,5},{5,6},{6,7},{7,0},{8,9},{9,10},{10,1... | collective-permute-start | bytes 786440 | tf_op jit(solution)/shard_map/ppermute | solution.py:13
  246.1 11.5 %collective-permute-start.5 = (bf16[16,16,512]{2,1,0:T(8,128)(2,1)S(1)}, bf16[16,16,512]{2,1,0:T(8,128)(2,1)S(1)}, u32[]{:S(2)}, u32[]{:S(2)}) collective-permute-start(bf16[16,16,512]{2,1,0:T(8,128)(2,1)S(1)} %collective-permute-done.4), channel_id=1, source_target_pairs={{0,7},{1,0},{2,1},{3,2},{4,3},{5,4},{6,5},{7,6},{8,15},{9,8},{10,9... | collective-permute-start | bytes 786440 | tf_op jit(solution)/shard_map/ppermute | solution.py:15
  249.7 18.0 %copy-start.5 = (bf16[16,16,512]{2,1,0:T(8,128)(2,1)}, bf16[16,16,512]{2,1,0:T(8,128)(2,1)S(1)}, u32[]{:S(2)}) copy-start(bf16[16,16,512]{2,1,0:T(8,128)(2,1)S(1)} %collective-permute-done.11) | copy-start | bytes 786436
  249.7 11.2 %collective-permute-start.12 = (bf16[16,16,512]{2,1,0:T(8,128)(2,1)S(1)}, bf16[16,16,512]{2,1,0:T(8,128)(2,1)}, u32[]{:S(2)}, u32[]{:S(2)}) collective-permute-start(bf16[16,16,512]{2,1,0:T(8,128)(2,1)S(1)} %collective-permute-done.11), channel_id=1, source_target_pairs={{0,7},{1,0},{2,1},{3,2},{4,3},{5,4},{6,5},{7,6},{8,15},{9,8},{10,9... | collective-permute-start | bytes 786440 | tf_op jit(solution)/shard_map/ppermute | solution.py:15
  253.4 14.3 %copy-start.7 = (bf16[16,16,512]{2,1,0:T(8,128)(2,1)}, bf16[16,16,512]{2,1,0:T(8,128)(2,1)S(1)}, u32[]{:S(2)}) copy-start(bf16[16,16,512]{2,1,0:T(8,128)(2,1)S(1)} %collective-permute-done.8) | copy-start | bytes 786436
  253.4 11.2 %collective-permute-start.9 = (bf16[16,16,512]{2,1,0:T(8,128)(2,1)S(1)}, bf16[16,16,512]{2,1,0:T(8,128)(2,1)}, u32[]{:S(2)}, u32[]{:S(2)}) collective-permute-start(bf16[16,16,512]{2,1,0:T(8,128)(2,1)S(1)} %collective-permute-done.8), channel_id=1, source_target_pairs={{0,1},{1,2},{2,3},{3,4},{4,5},{5,6},{6,7},{7,0},{8,9},{9,10},{10,1... | collective-permute-start | bytes 786440 | tf_op jit(solution)/shard_map/ppermute | solution.py:13
  257.2 9.3 %collective-permute-start.3 = (bf16[16,16,512]{2,1,0:T(8,128)(2,1)S(1)}, bf16[16,16,512]{2,1,0:T(8,128)(2,1)}, u32[]{:S(2)}, u32[]{:S(2)}) collective-permute-start(bf16[16,16,512]{2,1,0:T(8,128)(2,1)S(1)} %collective-permute-done.2), channel_id=1, source_target_pairs={{0,1},{1,2},{2,3},{3,4},{4,5},{5,6},{6,7},{7,0},{8,9},{9,10},{10,1... | collective-permute-start | bytes 786440 | tf_op jit(solution)/shard_map/ppermute | solution.py:13
  257.6 10.2 %copy-start.2 = (bf16[1,16,16,512]{3,2,1,0:T(8,128)(2,1)S(1)}, bf16[1,16,16,512]{3,2,1,0:T(8,128)(2,1)}, u32[]{:S(2)}) copy-start(bf16[1,16,16,512]{3,2,1,0:T(8,128)(2,1)} %get-tuple-element.17) | copy-start | bytes 786436
  257.6 10.1 %collective-permute-start.6 = (bf16[16,16,512]{2,1,0:T(8,128)(2,1)S(1)}, bf16[16,16,512]{2,1,0:T(8,128)(2,1)S(1)}, u32[]{:S(2)}, u32[]{:S(2)}) collective-permute-start(bf16[16,16,512]{2,1,0:T(8,128)(2,1)S(1)} %collective-permute-done.5), channel_id=1, source_target_pairs={{0,7},{1,0},{2,1},{3,2},{4,3},{5,4},{6,5},{7,6},{8,15},{9,8},{10,9... | collective-permute-start | bytes 786440 | tf_op jit(solution)/shard_map/ppermute | solution.py:15
  260.9 22.9 %collective-permute-start.13 = (bf16[16,16,512]{2,1,0:T(8,128)(2,1)}, bf16[16,16,512]{2,1,0:T(8,128)(2,1)}, u32[]{:S(2)}, u32[]{:S(2)}) collective-permute-start(bf16[16,16,512]{2,1,0:T(8,128)(2,1)} %collective-permute-done.12), channel_id=1, source_target_pairs={{0,7},{1,0},{2,1},{3,2},{4,3},{5,4},{6,5},{7,6},{8,15},{9,8},{10,9... | collective-permute-start | bytes 786440 | tf_op jit(solution)/shard_map/ppermute | solution.py:15
  264.7 7.8 %collective-permute-start.10 = (bf16[16,16,512]{2,1,0:T(8,128)(2,1)}, bf16[16,16,512]{2,1,0:T(8,128)(2,1)S(1)}, u32[]{:S(2)}, u32[]{:S(2)}) collective-permute-start(bf16[16,16,512]{2,1,0:T(8,128)(2,1)} %collective-permute-done.9), channel_id=1, source_target_pairs={{0,1},{1,2},{2,3},{3,4},{4,5},{5,6},{6,7},{7,0},{8,9},{9,10},{10,1... | collective-permute-start | bytes 786440 | tf_op jit(solution)/shard_map/ppermute | solution.py:13
  267.8 7.1 %copy-start.8 = (bf16[16,16,512]{2,1,0:T(8,128)(2,1)S(1)}, bf16[16,16,512]{2,1,0:T(8,128)(2,1)}, u32[]{:S(2)}) copy-start(bf16[16,16,512]{2,1,0:T(8,128)(2,1)} %copy-done.7) | copy-start | bytes 786436
  267.8 7.8 %copy-start.4 = (bf16[16,16,512]{2,1,0:T(8,128)(2,1)S(1)}, bf16[16,16,512]{2,1,0:T(8,128)(2,1)}, u32[]{:S(2)}) copy-start(bf16[16,16,512]{2,1,0:T(8,128)(2,1)} %copy-done.3) | copy-start | bytes 786436
  279.1 2.3 copy-start.6
Sparse Core Ops, SparseCore 0:
  9.8 56.2 all-gather.1
  144.2 78.5 all-reduce.2
  368.4 98.5 reduce-scatter.1
